TPU v7x, 32 devices: a whole 2x2x4 slice. The times are simulated.
32 devices in a mesh: dp: 8 (over y, x, core), mp: 4 (over z).
Axes of the slice: x: 2, y: 2, z: 4, core: 2. Of those that a mesh axis runs over, the one named last changes fastest.
Arguments:
- hidden_in: bfloat16 [4096, 2048], P('dp'), may hold values from -6 to 6
- cotangent: bfloat16 [4096, 2048], P('dp'), may hold values from -6 to 6
- segments: int32 [8, 512], P('dp'), may hold values from 0 to 5, never falling along the last dimension, each value on 1 to 256 neighbouring positions
- live_counts: int32 [8], P('dp'), may hold values from 128 to 512, as said below
- w_query: bfloat16 [2048, 2048], P('dp', 'mp'), may hold values from -0.125 to 0.125
- w_key: bfloat16 [2048, 2048], P('dp', 'mp'), may hold values from -0.125 to 0.125
- w_value: bfloat16 [2048, 2048], P('dp', 'mp'), may hold values from -0.125 to 0.125
- w_output: bfloat16 [2048, 2048], P('mp', 'dp'), may hold values from -0.125 to 0.125
- w_gate: bfloat16 [2048, 8192], P('dp', 'mp'), may hold values from -0.125 to 0.125
- w_up: bfloat16 [2048, 8192], P('dp', 'mp'), may hold values from -0.125 to 0.125
- w_down: bfloat16 [8192, 2048], P('mp', 'dp'), may hold values from -0.0625 to 0.0625
- query_gain: float32 [2048], P('mp'), may hold values from 0.5 to 1.5
- key_gain: float32 [2048], P('mp'), may hold values from 0.5 to 1.5
- attn_gain: float32 [2048], replicated, may hold values from 0.5 to 1.5
- ffn_gain: float32 [2048], replicated, may hold values from 0.5 to 1.5
Outputs:
- hidden_out: bfloat16 [4096, 2048], P('dp')
- grad_in: float32 [4096, 2048], P('dp')
- grad_query: float32 [2048, 2048], P('dp', 'mp')
- grad_key: float32 [2048, 2048], P('dp', 'mp')
- grad_value: float32 [2048, 2048], P('dp', 'mp')
- grad_output_w: float32 [2048, 2048], P('mp', 'dp')
- grad_gate: float32 [2048, 8192], P('dp', 'mp')
- grad_up: float32 [2048, 8192], P('dp', 'mp')
- grad_down: float32 [8192, 2048], P('mp', 'dp')
- grad_query_gain: float32 [2048], P('mp')
- grad_key_gain: float32 [2048], P('mp')
- grad_attn_gain: float32 [2048], replicated
- grad_ffn_gain: float32 [2048], replicated
Inputs may be any that keep to these rules, and one draw needn't show every extreme that they name: Within the rows of one index of dp, segments never fall; each of the 6 documents has 1 to 256 rows and one has exactly 256. `live_counts`: rows of a block at or after its live count are padding; some index of dp has 512 live rows and some has 128.
All inputs are finite; a program needn't handle non-finite values.
Results may differ from a plain program's by a relative error of at most 0.017.
Values may be sent and summed in bfloat16 or wider, within the bound.
A program may use at most 256 MiB of HBM per device.

v0:
```python
import math
import jax
import jax.numpy as jnp
from jax import lax
from jax.sharding import PartitionSpec as P

HD = 128
EPS = 1e-06
THETA = 500000.0


def doc_positions(seg_row):
    row_count = seg_row.shape[0]
    row_index = jnp.arange(row_count, dtype=jnp.int32)
    change = jnp.concatenate([jnp.ones((1,), dtype=bool), seg_row[1:] != seg_row[:-1]])
    doc_start = lax.cummax(jnp.where(change, row_index, jnp.zeros_like(row_index)), axis=0)
    return (row_index - doc_start).astype(jnp.float32)


def rotary_tables(positions, head_size):
    half_size = head_size // 2
    inv_freq = THETA ** (-(jnp.arange(half_size, dtype=jnp.float32) * (2.0 / head_size)))
    angles = positions[:, None] * inv_freq[None, :]
    return (jnp.cos(angles)[:, None, :], jnp.sin(angles)[:, None, :])


def rotate(values, cos_tab, sin_tab):
    half_size = values.shape[2] // 2
    first_half = values[:, :, :half_size]
    second_half = values[:, :, half_size:]
    return jnp.concatenate(
        [
            first_half * cos_tab - second_half * sin_tab,
            second_half * cos_tab + first_half * sin_tab,
        ],
        axis=2,
    )


def rotate_back(grads, cos_tab, sin_tab):
    half_size = grads.shape[2] // 2
    first_half = grads[:, :, :half_size]
    second_half = grads[:, :, half_size:]
    return jnp.concatenate(
        [
            first_half * cos_tab + second_half * sin_tab,
            second_half * cos_tab - first_half * sin_tab,
        ],
        axis=2,
    )


def block_mask(seg_row, offset, block_rows):
    row_index = jnp.arange(seg_row.shape[0])
    same = seg_row[offset : offset + block_rows, None] == seg_row[None, :]
    return same & (row_index[:, None] >= row_index[None, :])


def block_scores(q_blk, k_bf, allowed, score_scale):
    scores = (
        jnp.einsum("qhe,khe->hqk", q_blk, k_bf, preferred_element_type=jnp.float32) * score_scale
    )
    return jnp.where(allowed[None], scores, jnp.float32(-1e30))


def attend_forward(q_bf, k_bf, v_bf, seg_row, score_scale):
    row_count = q_bf.shape[0]
    block_rows = min(512, row_count)
    allowed = block_mask(seg_row, 0, block_rows)
    scores = block_scores(q_bf, k_bf, allowed, score_scale)
    row_max = jnp.max(scores, axis=2, keepdims=True)
    lse = row_max + jnp.log(jnp.sum(jnp.exp(scores - row_max), axis=2, keepdims=True))
    probs = jnp.exp(scores - lse).astype(jnp.bfloat16)
    outputs = jnp.einsum("hqk,khe->qhe", probs, v_bf, preferred_element_type=jnp.float32)
    lse_parts = [lse]
    return (outputs.astype(jnp.bfloat16), lse_parts)


def attend_backward(q_bf, k_bf, v_bf, o_bf, do_bf, lse_parts, seg_row, score_scale):
    row_count = q_bf.shape[0]
    block_rows = min(512, row_count)
    dq_parts = []
    dk_acc = jnp.zeros(k_bf.shape, jnp.float32)
    dv_acc = jnp.zeros(v_bf.shape, jnp.float32)
    for part_index, offset in enumerate(range(0, row_count, block_rows)):
        allowed = block_mask(seg_row, offset, block_rows)
        scores = block_scores(q_bf, k_bf, allowed, score_scale)
        probs = jnp.exp(scores - lse_parts[part_index])
        probs_bf = probs.astype(jnp.bfloat16)
        dprob = jnp.einsum("qhe,khe->hqk", do_bf, v_bf, preferred_element_type=jnp.float32)
        delta = jnp.transpose(
            jnp.sum(do_bf.astype(jnp.float32) * o_bf.astype(jnp.float32), axis=2)
        )[:, :, None]
        dscore = (probs * (dprob - delta)).astype(jnp.bfloat16)
        dq_parts.append(
            jnp.einsum("hqk,khe->qhe", dscore, k_bf, preferred_element_type=jnp.float32)
            * score_scale
        )
        dk_acc = (
            jnp.einsum("hqk,qhe->khe", dscore, q_bf, preferred_element_type=jnp.float32)
            * score_scale
        )
        dv_acc = jnp.einsum("hqk,qhe->khe", probs_bf, do_bf, preferred_element_type=jnp.float32)
    return (dq_parts[0], dk_acc, dv_acc.astype(jnp.bfloat16))


def scatter_grad(grad, axis_name, scatter_dimension, tiled):
    total = lax.psum_scatter(
        grad.astype(jnp.bfloat16), axis_name, scatter_dimension=scatter_dimension, tiled=tiled
    )
    return total.astype(jnp.float32)


def sum_parts(part, axis_name):
    own = lax.psum_scatter(part.astype(jnp.bfloat16), axis_name, scatter_dimension=0, tiled=True)
    return lax.all_gather(own, axis_name, axis=0, tiled=True).astype(jnp.float32)


def norm_back(raw, inv_scale, gained, row_sums, width):
    return inv_scale * gained - raw * inv_scale**3 * (row_sums[:, None] / width)


def on_device(
    hidden_in,
    cotangent,
    segments,
    live_counts,
    w_query,
    w_key,
    w_value,
    w_output,
    w_gate,
    w_up,
    w_down,
    query_gain,
    key_gain,
    attn_gain,
    ffn_gain,
):
    gathered = (
        lax.all_gather(w_query, "dp", axis=0, tiled=True),
        lax.all_gather(w_key, "dp", axis=0, tiled=True),
        lax.all_gather(w_value, "dp", axis=0, tiled=True),
        lax.all_gather(w_output, "dp", axis=1, tiled=True),
        lax.all_gather(w_gate, "dp", axis=0, tiled=True),
        lax.all_gather(w_up, "dp", axis=0, tiled=True),
        lax.all_gather(w_down, "dp", axis=1, tiled=True),
    )
    wq_full, wk_full, wv_full, wo_full, wg_full, wu_full, wd_full = gathered
    seg_row = segments[0]
    live_n = live_counts[0]
    row_count, width = hidden_in.shape
    local_width = wq_full.shape[1]
    heads_here = local_width // HD
    score_scale = 1.0 / math.sqrt(HD)
    live_mask = (jnp.arange(row_count, dtype=jnp.int32) < live_n).astype(jnp.float32)[:, None]
    cos_tab, sin_tab = rotary_tables(doc_positions(seg_row), HD)
    q_proj = jnp.dot(hidden_in, wq_full, preferred_element_type=jnp.float32)
    k_proj = jnp.dot(hidden_in, wk_full, preferred_element_type=jnp.float32)
    v_bf = jnp.dot(hidden_in, wv_full, preferred_element_type=jnp.float32).astype(jnp.bfloat16)
    sq_query, sq_key = lax.psum(
        (jnp.sum(q_proj * q_proj, axis=1), jnp.sum(k_proj * k_proj, axis=1)), "mp"
    )
    inv_q = lax.rsqrt(sq_query[:, None] / width + EPS)
    inv_k = lax.rsqrt(sq_key[:, None] / width + EPS)
    q_rot = rotate(
        (q_proj * inv_q * query_gain).reshape(row_count, heads_here, HD), cos_tab, sin_tab
    ).astype(jnp.bfloat16)
    k_rot = rotate(
        (k_proj * inv_k * key_gain).reshape(row_count, heads_here, HD), cos_tab, sin_tab
    ).astype(jnp.bfloat16)
    v_heads = v_bf.reshape(row_count, heads_here, HD)
    o_bf, lse_parts = attend_forward(q_rot, k_rot, v_heads, seg_row, score_scale)
    o_flat = o_bf.reshape(row_count, local_width)
    attn_raw = sum_parts(jnp.dot(o_flat, wo_full, preferred_element_type=jnp.float32), "mp")
    inv_a = lax.rsqrt(jnp.mean(attn_raw * attn_raw, axis=1, keepdims=True) + EPS)
    h_mid = hidden_in.astype(jnp.float32) + attn_raw * inv_a * attn_gain
    h_bf = h_mid.astype(jnp.bfloat16)
    gate_pre = jnp.dot(h_bf, wg_full, preferred_element_type=jnp.float32)
    up_pre = jnp.dot(h_bf, wu_full, preferred_element_type=jnp.float32)
    act_bf = (jax.nn.silu(gate_pre) * up_pre).astype(jnp.bfloat16)
    ffn_raw = sum_parts(jnp.dot(act_bf, wd_full, preferred_element_type=jnp.float32), "mp")
    inv_f = lax.rsqrt(jnp.mean(ffn_raw * ffn_raw, axis=1, keepdims=True) + EPS)
    hidden_out = (live_mask * (h_mid + ffn_raw * inv_f * ffn_gain)).astype(jnp.bfloat16)
    wq_back, wk_back, wv_back, wo_back, wg_back, wu_back, wd_back = gathered
    dy = live_mask * cotangent.astype(jnp.float32)
    g_ffn_gain = jnp.sum(dy * ffn_raw * inv_f, axis=0)
    gained_f = ffn_gain * dy
    d_ffn = norm_back(ffn_raw, inv_f, gained_f, jnp.sum(gained_f * ffn_raw, axis=1), width).astype(
        jnp.bfloat16
    )
    d_act = jnp.dot(d_ffn, wd_back.T, preferred_element_type=jnp.float32)
    sig = jax.nn.sigmoid(gate_pre)
    d_up = (d_act * gate_pre * sig).astype(jnp.bfloat16)
    d_gate = (d_act * up_pre * sig * (1.0 + gate_pre * (1.0 - sig))).astype(jnp.bfloat16)
    ffn_part = jnp.dot(d_gate, wg_back.T, preferred_element_type=jnp.float32) + jnp.dot(
        d_up, wu_back.T, preferred_element_type=jnp.float32
    )
    dh = dy + sum_parts(ffn_part, "mp")
    g_down = jnp.dot(act_bf.T, d_ffn, preferred_element_type=jnp.float32)
    g_gate = jnp.dot(h_bf.T, d_gate, preferred_element_type=jnp.float32)
    g_up = jnp.dot(h_bf.T, d_up, preferred_element_type=jnp.float32)
    g_attn_gain = jnp.sum(dh * attn_raw * inv_a, axis=0)
    gained_a = attn_gain * dh
    d_attn = norm_back(
        attn_raw, inv_a, gained_a, jnp.sum(gained_a * attn_raw, axis=1), width
    ).astype(jnp.bfloat16)
    d_heads = jnp.dot(d_attn, wo_back.T, preferred_element_type=jnp.float32).astype(jnp.bfloat16)
    g_output = jnp.dot(o_flat.T, d_attn, preferred_element_type=jnp.float32)
    dq_rot, dk_rot, d_val = attend_backward(
        q_rot,
        k_rot,
        v_heads,
        o_bf,
        d_heads.reshape(row_count, heads_here, HD),
        lse_parts,
        seg_row,
        score_scale,
    )
    dq_norm = rotate_back(dq_rot, cos_tab, sin_tab).reshape(row_count, local_width)
    dk_norm = rotate_back(dk_rot, cos_tab, sin_tab).reshape(row_count, local_width)
    g_query_gain = jnp.sum(dq_norm * q_proj * inv_q, axis=0)
    g_key_gain = jnp.sum(dk_norm * k_proj * inv_k, axis=0)
    gained_q = query_gain * dq_norm
    gained_k = key_gain * dk_norm
    sums_query, sums_key = lax.psum(
        (jnp.sum(gained_q * q_proj, axis=1), jnp.sum(gained_k * k_proj, axis=1)), "mp"
    )
    dq_bf = norm_back(q_proj, inv_q, gained_q, sums_query, width).astype(jnp.bfloat16)
    dk_bf = norm_back(k_proj, inv_k, gained_k, sums_key, width).astype(jnp.bfloat16)
    dv_bf = d_val.reshape(row_count, local_width)
    input_part = (
        jnp.dot(dq_bf, wq_back.T, preferred_element_type=jnp.float32)
        + jnp.dot(dk_bf, wk_back.T, preferred_element_type=jnp.float32)
        + jnp.dot(dv_bf, wv_back.T, preferred_element_type=jnp.float32)
    )
    grad_in = dh + sum_parts(input_part, "mp")
    g_query = jnp.dot(hidden_in.T, dq_bf, preferred_element_type=jnp.float32)
    g_key = jnp.dot(hidden_in.T, dk_bf, preferred_element_type=jnp.float32)
    g_value = jnp.dot(hidden_in.T, dv_bf, preferred_element_type=jnp.float32)
    owned = (
        scatter_grad(g_query, "dp", scatter_dimension=0, tiled=True),
        scatter_grad(g_key, "dp", scatter_dimension=0, tiled=True),
        scatter_grad(g_value, "dp", scatter_dimension=0, tiled=True),
        scatter_grad(g_output, "dp", scatter_dimension=1, tiled=True),
        scatter_grad(g_gate, "dp", scatter_dimension=0, tiled=True),
        scatter_grad(g_up, "dp", scatter_dimension=0, tiled=True),
        scatter_grad(g_down, "dp", scatter_dimension=1, tiled=True),
    )
    gain_totals = lax.psum((g_query_gain, g_key_gain, g_attn_gain, g_ffn_gain), "dp")
    return (
        hidden_out,
        grad_in,
        owned[0],
        owned[1],
        owned[2],
        owned[3],
        owned[4],
        owned[5],
        owned[6],
        gain_totals[0],
        gain_totals[1],
        gain_totals[2],
        gain_totals[3],
    )


def solution(mesh):
    return jax.shard_map(
        on_device,
        mesh=mesh,
        in_specs=(
            P("dp", None),
            P("dp", None),
            P("dp", None),
            P("dp"),
            P("dp", "mp"),
            P("dp", "mp"),
            P("dp", "mp"),
            P("mp", "dp"),
            P("dp", "mp"),
            P("dp", "mp"),
            P("mp", "dp"),
            P("mp"),
            P("mp"),
            P(),
            P(),
        ),
        out_specs=(
            P("dp", None),
            P("dp", None),
            P("dp", "mp"),
            P("dp", "mp"),
            P("dp", "mp"),
            P("mp", "dp"),
            P("dp", "mp"),
            P("dp", "mp"),
            P("mp", "dp"),
            P("mp"),
            P("mp"),
            P(),
            P(),
        ),
        check_vma=False,
    )
```

profile of v0, /device:TPU:0, one launch (start us, length us, event | category | flops | bytes accessed | tf_op | source)
XLA Modules:
  0.0 1167.2 jit_solution(17144449254800355425)
XLA Ops:
  14.4 26.0 %all-gather.16.cloned.1.call-done = bf16[2048,512]{1,0:T(8,128)(2,1)} async-done(((bf16[256,512]{1,0:T(8,128)(2,1)}), bf16[2048,512]{1,0:T(8,128)(2,1)}) %all-gather.16.cloned.1.call-update) | async-done | bytes 2097168 | tf_op jit(solution)/shard_map/all_gather | solution.py:142
  44.0 26.1 %all-gather.14.cloned.1.call-done = bf16[2048,512]{1,0:T(8,128)(2,1)} async-done(((bf16[256,512]{1,0:T(8,128)(2,1)}), bf16[2048,512]{1,0:T(8,128)(2,1)}) %all-gather.14.cloned.1.call-update) | async-done | bytes 2097168 | tf_op jit(solution)/shard_map/all_gather | solution.py:141
  73.7 11.7 %all-reduce.2 = (f32[512]{0:T(512)S(1)}, f32[512]{0:T(512)S(1)}) all-reduce(f32[512]{0:T(512)S(1)} %get-tuple-element.85, f32[512]{0:T(512)S(1)} %get-tuple-element.87), channel_id=1, replica_groups=mesh['dp'=8,'mp'=4] {'mp'}, use_global_device_ids=true, to_apply=%region_5.6 | all-reduce | flops 1024 | bytes 8192 | tf_op jit(solution)/shard_map/psum | solution.py:161
  109.1 20.6 %all-gather.18.cloned.1.call-done = bf16[512,2048]{1,0:T(8,128)(2,1)} async-done(((bf16[512,256]{1,0:T(8,128)(2,1)}), bf16[512,2048]{1,0:T(8,128)(2,1)}) %all-gather.18.cloned.1.call-update) | async-done | bytes 2097168 | tf_op jit(solution)/shard_map/all_gather | solution.py:144
  134.1 43.7 %reduce-scatter.12.cloned.1.call-done = bf16[128,2048]{1,0:T(8,128)(2,1)} async-done(((bf16[512,2048]{1,0:T(8,128)(2,1)}), bf16[128,2048]{1,0:T(8,128)(2,1)}) %reduce-scatter.12.cloned.1.call-update) | async-done | bytes 524304 | tf_op jit(solution)/shard_map/reduce_scatter | solution.py:115
  180.2 44.0 %all-gather.20.cloned.1.call-done = bf16[512,2048]{1,0:T(8,128)(2,1)} async-done(((bf16[128,2048]{1,0:T(8,128)(2,1)}), bf16[512,2048]{1,0:T(8,128)(2,1)}) %all-gather.20.cloned.1.call-update) | async-done | bytes 2097168 | tf_op jit(solution)/shard_map/all_gather | solution.py:116
  230.3 48.9 %all-gather.22.cloned.1.call-done = bf16[2048,2048]{1,0:T(8,128)(2,1)} async-done(((bf16[256,2048]{1,0:T(8,128)(2,1)}), bf16[2048,2048]{1,0:T(8,128)(2,1)}) %all-gather.22.cloned.1.call-update) | async-done | bytes 8388624 | tf_op jit(solution)/shard_map/all_gather | solution.py:145
  289.6 45.7 %all-gather.24.cloned.1.call-done = bf16[2048,2048]{1,0:T(8,128)(2,1)} async-done(((bf16[256,2048]{1,0:T(8,128)(2,1)}), bf16[2048,2048]{1,0:T(8,128)(2,1)}) %all-gather.24.cloned.1.call-update) | async-done | bytes 8388624 | tf_op jit(solution)/shard_map/all_gather | solution.py:146
  335.3 10.8 multiply_convert_fusion.3
  346.1 47.0 %all-gather.26.cloned.1.call-done = bf16[2048,2048]{1,0:T(8,128)(2,1)} async-done(((bf16[2048,256]{1,0:T(8,128)(2,1)}), bf16[2048,2048]{1,0:T(8,128)(2,1)}) %all-gather.26.cloned.1.call-update) | async-done | bytes 8388624 | tf_op jit(solution)/shard_map/all_gather | solution.py:147
  403.0 43.7 %reduce-scatter.14.cloned.1.call-done = bf16[128,2048]{1,0:T(8,128)(2,1)} async-done(((bf16[512,2048]{1,0:T(8,128)(2,1)}), bf16[128,2048]{1,0:T(8,128)(2,1)}) %reduce-scatter.14.cloned.1.call-update) | async-done | bytes 524304 | tf_op jit(solution)/shard_map/reduce_scatter | solution.py:115
  447.7 45.6 %all-gather.28.cloned.1.call-done = bf16[512,2048]{1,0:T(8,128)(2,1)} async-done(((bf16[128,2048]{1,0:T(8,128)(2,1)}), bf16[512,2048]{1,0:T(8,128)(2,1)}) %all-gather.28.cloned.1.call-update) | async-done | bytes 2097168 | tf_op jit(solution)/shard_map/all_gather | solution.py:116
  498.9 11.9 %multiply_convert_fusion.1 = (bf16[512,2048]{1,0:T(8,128)(2,1)}, bf16[512,2048]{1,0:T(8,128)(2,1)}) fusion(f32[512,2048]{1,0:T(8,128)S(1)} %copy-done.45, f32[512,2048]{1,0:T(8,128)} %get-tuple-element.92, bf16[2048,2048]{1,0:T(8,128)(2,1)} %all-gather.26.cloned.1.call-done, bf16[512,2048]{1,0:T(8,128)(2,1)S(1)} %copy-done.5, ...), kind=kOutput, calls=%fused_computation.38 | convolution fusion | flops 4318035968 | bytes 25182208 | tf_op jit(solution)/shard_map/dot_general | solution.py:192
  528.2 42.5 %reduce-scatter.16.cloned.1.call-done = bf16[128,2048]{1,0:T(8,128)(2,1)} async-done(((bf16[512,2048]{1,0:T(8,128)(2,1)}), bf16[128,2048]{1,0:T(8,128)(2,1)}) %reduce-scatter.16.cloned.1.call-update) | async-done | bytes 524304 | tf_op jit(solution)/shard_map/reduce_scatter | solution.py:115
  571.0 46.2 %all-gather.30.cloned.1.call-done = bf16[512,2048]{1,0:T(8,128)(2,1)} async-done(((bf16[128,2048]{1,0:T(8,128)(2,1)}), bf16[512,2048]{1,0:T(8,128)(2,1)}) %all-gather.30.cloned.1.call-update) | async-done | bytes 2097168 | tf_op jit(solution)/shard_map/all_gather | solution.py:116
  710.4 23.1 %all-reduce = (f32[512]{0:T(512)}, f32[512]{0:T(512)}, f32[2048]{0:T(1024)}, f32[2048]{0:T(1024)}) all-reduce(f32[512]{0:T(512)S(1)} %get-tuple-element.45, f32[512]{0:T(512)S(1)} %get-tuple-element.43, f32[2048]{0:T(1024)S(1)} %get-tuple-element.39, f32[2048]{0:T(1024)S(1)} %get-tuple-element.41), channel_id=1, replica_groups=mesh['dp'=8,'mp'=4] {'dp'}, use_global_device_ids=true, to_apply=%region_29.30 | all-reduce | flops 5120 | bytes 40960 | tf_op jit(solution)/shard_map/psum | solution.py:250
  733.5 16.2 %reduce-scatter.26.cloned.1.call-done = bf16[512,256]{1,0:T(8,128)(2,1)} async-done(((bf16[512,2048]{1,0:T(8,128)(2,1)}), bf16[512,256]{1,0:T(8,128)(2,1)}) %reduce-scatter.26.cloned.1.call-update) | async-done | bytes 262160 | tf_op jit(solution)/shard_map/reduce_scatter | solution.py:108
  751.4 42.5 %reduce-scatter.22.cloned.1.call-done = bf16[256,512]{0,1:T(8,128)(2,1)} async-done(((bf16[2048,512]{0,1:T(8,128)(2,1)}), bf16[256,512]{0,1:T(8,128)(2,1)}) %reduce-scatter.22.cloned.1.call-update) | async-done | bytes 262160 | tf_op jit(solution)/shard_map/reduce_scatter | solution.py:108
  795.9 42.4 %reduce-scatter.20.cloned.1.call-done = bf16[256,512]{0,1:T(8,128)(2,1)} async-done(((bf16[2048,512]{0,1:T(8,128)(2,1)}), bf16[256,512]{0,1:T(8,128)(2,1)}) %reduce-scatter.20.cloned.1.call-update) | async-done | bytes 262160 | tf_op jit(solution)/shard_map/reduce_scatter | solution.py:108
  840.1 42.4 %reduce-scatter.24.cloned.1.call-done = bf16[256,512]{0,1:T(8,128)(2,1)} async-done(((bf16[2048,512]{0,1:T(8,128)(2,1)}), bf16[256,512]{0,1:T(8,128)(2,1)}) %reduce-scatter.24.cloned.1.call-update) | async-done | bytes 262160 | tf_op jit(solution)/shard_map/reduce_scatter | solution.py:108
  884.4 72.9 %reduce-scatter.32.cloned.1.call-done = bf16[2048,256]{1,0:T(8,128)(2,1)} async-done(((bf16[2048,2048]{1,0:T(8,128)(2,1)}), bf16[2048,256]{1,0:T(8,128)(2,1)}) %reduce-scatter.32.cloned.1.call-update) | async-done | bytes 1048592 | tf_op jit(solution)/shard_map/reduce_scatter | solution.py:108
  960.1 72.2 %reduce-scatter.30.cloned.1.call-done = bf16[256,2048]{1,0:T(8,128)(2,1)} async-done(((bf16[2048,2048]{1,0:T(8,128)(2,1)}), bf16[256,2048]{1,0:T(8,128)(2,1)}) %reduce-scatter.30.cloned.1.call-update) | async-done | bytes 1048592 | tf_op jit(solution)/shard_map/reduce_scatter | solution.py:108
  1035.0 72.2 %reduce-scatter.28.cloned.1.call-done = bf16[256,2048]{1,0:T(8,128)(2,1)} async-done(((bf16[2048,2048]{1,0:T(8,128)(2,1)}), bf16[256,2048]{1,0:T(8,128)(2,1)}) %reduce-scatter.28.cloned.1.call-update) | async-done | bytes 1048592 | tf_op jit(solution)/shard_map/reduce_scatter | solution.py:108
  1110.0 44.5 %all-gather.32.cloned.1.call-done = bf16[512,2048]{1,0:T(8,128)(2,1)} async-done(((bf16[128,2048]{1,0:T(8,128)(2,1)}), bf16[512,2048]{1,0:T(8,128)(2,1)}) %all-gather.32.cloned.1.call-update) | async-done | bytes 2097168 | tf_op jit(solution)/shard_map/all_gather | solution.py:116
  (218 shorter events, 208.5 us)
Async XLA Ops:
  7.2 33.2 %all-gather.16.cloned.1.call-start = ((), (), s32[]{:S(2)}) async-start(), calls=%async_computation.13 | async-start | bytes 2359296 | tf_op jit(solution)/shard_map/all_gather | solution.py:142
  7.9 62.2 %all-gather.14.cloned.1.call-start = ((), (), s32[]{:S(2)}) async-start(), calls=%async_computation.12 | async-start | bytes 2359296 | tf_op jit(solution)/shard_map/all_gather | solution.py:141
  8.7 94.4 %all-gather.12.cloned.1.call-start = ((), (), s32[]{:S(2)}) async-start(), calls=%async_computation.11 | async-start | bytes 2359296 | tf_op jit(solution)/shard_map/all_gather | solution.py:143
  9.4 120.3 %all-gather.18.cloned.1.call-start = ((), (), s32[]{:S(2)}) async-start(), calls=%async_computation.14 | async-start | bytes 2359296 | tf_op jit(solution)/shard_map/all_gather | solution.py:144
  10.0 167.9 %reduce-scatter.12.cloned.1.call-start = ((), (), s32[]{:S(2)}) async-start(), calls=%async_computation.15 | async-start | bytes 2621440 | tf_op jit(solution)/shard_map/reduce_scatter | solution.py:115
  134.1 90.1 %all-gather.20.cloned.1.call-start = ((), (), s32[]{:S(2)}) async-start(), calls=%async_computation.16 | async-start | bytes 2621440 | tf_op jit(solution)/shard_map/all_gather | solution.py:116
  177.9 101.3 %all-gather.22.cloned.1.call-start = ((), (), s32[]{:S(2)}) async-start(), calls=%async_computation.17 | async-start | bytes 9437184 | tf_op jit(solution)/shard_map/all_gather | solution.py:145
  178.6 156.7 %all-gather.24.cloned.1.call-start = ((), (), s32[]{:S(2)}) async-start(), calls=%async_computation.18 | async-start | bytes 9437184 | tf_op jit(solution)/shard_map/all_gather | solution.py:146
  179.4 213.7 %all-gather.26.cloned.1.call-start = ((), (), s32[]{:S(2)}) async-start(), calls=%async_computation.19 | async-start | bytes 9437184 | tf_op jit(solution)/shard_map/all_gather | solution.py:147
  180.1 266.6 %reduce-scatter.14.cloned.1.call-start = ((), (), s32[]{:S(2)}) async-start(), calls=%async_computation.20 | async-start | bytes 2621440 | tf_op jit(solution)/shard_map/reduce_scatter | solution.py:115
  230.3 105.1 %copy-start.30 = (bf16[512,2048]{1,0:T(8,128)(2,1)S(1)}, bf16[512,2048]{1,0:T(8,128)(2,1)}, u32[]{:S(2)}) copy-start(bf16[512,2048]{1,0:T(8,128)(2,1)} %fusion.22) | copy-start | bytes 6291460
  403.0 90.3 %all-gather.28.cloned.1.call-start = ((), (), s32[]{:S(2)}) async-start(), calls=%async_computation.21 | async-start | bytes 2621440 | tf_op jit(solution)/shard_map/all_gather | solution.py:116
  446.8 124.0 %reduce-scatter.16.cloned.1.call-start = ((), (), s32[]{:S(2)}) async-start(), calls=%async_computation.22 | async-start | bytes 2621440 | tf_op jit(solution)/shard_map/reduce_scatter | solution.py:115
  518.6 98.6 %copy-start = (bf16[512,2048]{1,0:T(8,128)(2,1)S(1)}, bf16[512,2048]{1,0:T(8,128)(2,1)}, u32[]{:S(2)}) copy-start(bf16[512,2048]{1,0:T(8,128)(2,1)} %all-gather.20.cloned.1.call-done) | copy-start | bytes 6291460
  528.2 89.0 %all-gather.30.cloned.1.call-start = ((), (), s32[]{:S(2)}) async-start(), calls=%async_computation.23 | async-start | bytes 2621440 | tf_op jit(solution)/shard_map/all_gather | solution.py:116
  570.8 139.0 %reduce-scatter.18.cloned.1.call-start = ((), (), s32[]{:S(2)}) async-start(), calls=%async_computation.24 | async-start | bytes 2621440 | tf_op jit(solution)/shard_map/reduce_scatter | solution.py:115
  664.2 85.5 %reduce-scatter.26.cloned.1.call-start = ((), (), s32[]{:S(2)}) async-start(), calls=%async_computation.29 | async-start | bytes 2359296 | tf_op jit(solution)/shard_map/reduce_scatter | solution.py:108
  668.7 125.3 %reduce-scatter.22.cloned.1.call-start = ((), (), s32[]{:S(2)}) async-start(), calls=%async_computation.27 | async-start | bytes 2359296 | tf_op jit(solution)/shard_map/reduce_scatter | solution.py:108
  671.3 166.9 %reduce-scatter.20.cloned.1.call-start = ((), (), s32[]{:S(2)}) async-start(), calls=%async_computation.26 | async-start | bytes 2359296 | tf_op jit(solution)/shard_map/reduce_scatter | solution.py:108
  674.0 208.6 %reduce-scatter.24.cloned.1.call-start = ((), (), s32[]{:S(2)}) async-start(), calls=%async_computation.28 | async-start | bytes 2359296 | tf_op jit(solution)/shard_map/reduce_scatter | solution.py:108
  678.4 278.9 %reduce-scatter.32.cloned.1.call-start = ((), (), s32[]{:S(2)}) async-start(), calls=%async_computation.32 | async-start | bytes 9437184 | tf_op jit(solution)/shard_map/reduce_scatter | solution.py:108
  689.2 343.1 %reduce-scatter.30.cloned.1.call-start = ((), (), s32[]{:S(2)}) async-start(), calls=%async_computation.31 | async-start | bytes 9437184 | tf_op jit(solution)/shard_map/reduce_scatter | solution.py:108
  699.3 407.9 %reduce-scatter.28.cloned.1.call-start = ((), (), s32[]{:S(2)}) async-start(), calls=%async_computation.30 | async-start | bytes 9437184 | tf_op jit(solution)/shard_map/reduce_scatter | solution.py:108
  709.7 444.8 %all-gather.32.cloned.1.call-start = ((), (), s32[]{:S(2)}) async-start(), calls=%async_computation.25 | async-start | bytes 2621440 | tf_op jit(solution)/shard_map/all_gather | solution.py:116
  (45 other events, 490.0 us)
Sparse Core Ops, SparseCore 0:
  9.9 30.4 all-gather.15
  42.3 27.7 all-gather.13
  72.0 27.7 all-gather.11
  101.5 28.0 all-gather.17
  134.2 43.6 reduce-scatter.11
  179.3 44.8 all-gather.19
  226.1 53.0 all-gather.21
  281.0 54.2 all-gather.23
  337.2 55.8 all-gather.25
  403.1 43.6 reduce-scatter.13
  448.3 44.8 all-gather.27
  528.3 42.4 reduce-scatter.15
  572.3 44.8 all-gather.29
  664.3 41.8 reduce-scatter.17
  709.3 40.3 reduce-scatter.25
  752.8 41.1 reduce-scatter.21
  797.1 41.1 reduce-scatter.19
  841.4 41.1 reduce-scatter.23
  886.0 71.2 reduce-scatter.31
  960.7 71.5 reduce-scatter.29
  1035.7 71.4 reduce-scatter.27
  1108.8 45.6 all-gather.31
where the time goes:
time: 1180 us; the launch traced here: 1170 us
  waiting for transfers between devices  891 us (76%)
  matrix products  135 us (11%)
  other arithmetic  53.6 us (5%)
  blocking collectives  44.9 us (4%)
  local copies, waits for them, and re-layouts  25 us (2%)
  between operations  15.9 us (1%)
    reduce_scatter x7, waiting for transfers between devices, scatter_grad(): lax.psum_scatter(grad.astype(jnp.bfloat16), axis_name, scatter_dimension=...  361 us
    all_gather x4, waiting for transfers between devices, sum_parts(): lax.all_gather(own, axis_name, axis=0, tiled=True).astype(jnp.float32)  180 us
    reduce_scatter x4, waiting for transfers between devices, sum_parts(): lax.psum_scatter(part.astype(jnp.bfloat16), axis_name, scatter_dimension=...  130 us
    all_gather x1, waiting for transfers between devices, on_device(): lax.all_gather(w_gate, 'dp', axis=0, tiled=True)  48.9 us
    all_gather x1, waiting for transfers between devices, on_device(): lax.all_gather(w_down, 'dp', axis=1, tiled=True)  47 us
    all_gather x1, waiting for transfers between devices, on_device(): lax.all_gather(w_up, 'dp', axis=0, tiled=True)  45.7 us
    all_gather x1, waiting for transfers between devices, on_device(): lax.all_gather(w_query, 'dp', axis=0, tiled=True)  26.1 us
    all_gather x1, waiting for transfers between devices, on_device(): lax.all_gather(w_key, 'dp', axis=0, tiled=True)  26 us
  transfers between devices with their start and end apart: 22, of which 20 were waited for; matrix products, arithmetic and copies ran while one was open for 10% of the time, Pallas kernels for 0%

commit v1 on v0

--- a/solution.py
+++ b/solution.py
@@ -113,7 +113,9 @@
 
 def sum_parts(part, axis_name):
     own = lax.psum_scatter(part.astype(jnp.bfloat16), axis_name, scatter_dimension=0, tiled=True)
-    return lax.all_gather(own, axis_name, axis=0, tiled=True).astype(jnp.float32)
+    return jnp.concatenate(
+        lax.all_to_all(jnp.stack([own] * lax.axis_size(axis_name)), axis_name, 0, 0), axis=0
+    ).astype(jnp.float32)
 
 
 def norm_back(raw, inv_scale, gained, row_sums, width):

time: 1180 us -> 1110 us (0.941)
  waiting for transfers between devices: 891 us -> 742 us
  blocking collectives: 44.9 us -> 97.3 us
  starting transfers between devices: 2.11 us -> 15.4 us
    all_gather x4 -> x0, waiting for transfers between devices: 180 us -> none  [sum_parts(): lax.all_gather(own, axis_name, axis=0, tiled=True).astype(jnp.float32)]
    all_to_all x0 -> x3, waiting for transfers between devices: none -> 95.1 us  [sum_parts(): lax.all_to_all(jnp.stack([own] * lax.axis_size(axis_name)), axis_name, 0, 0)]
    all_to_all x0 -> x1, blocking collectives: none -> 51.2 us  [sum_parts(): lax.all_to_all(jnp.stack([own] * lax.axis_size(axis_name)), axis_name, 0, 0)]
    all_gather x1, waiting for transfers between devices: 48.9 us -> 0.01 us  [on_device(): lax.all_gather(w_gate, 'dp', axis=0, tiled=True)]
    all_to_all x0 -> x3, starting transfers between devices: none -> 13.5 us  [sum_parts(): lax.all_to_all(jnp.stack([own] * lax.axis_size(axis_name)), axis_name, 0, 0)]
  transfers between devices with their start and end apart: 22 -> 21, of which waited for: 20 -> 17; matrix products, arithmetic and copies ran while one was open for 10% -> 11% of each run, Pallas kernels for 0% -> 0%
where the time goes in v1:
time: 1110 us; the launch traced here: 1100 us
  waiting for transfers between devices  742 us (67%)
  matrix products  137 us (12%)
  blocking collectives  97.3 us (9%)
  other arithmetic  59.6 us (5%)
  local copies, waits for them, and re-layouts  36.2 us (3%)
  between operations  15.9 us (1%)
  starting transfers between devices  15.4 us (1%)
    reduce_scatter x7, waiting for transfers between devices, scatter_grad(): lax.psum_scatter(grad.astype(jnp.bfloat16), axis_name, scatter_dimension=...  351 us
    reduce_scatter x4, waiting for transfers between devices, sum_parts(): lax.psum_scatter(part.astype(jnp.bfloat16), axis_name, scatter_dimension=...  128 us
    all_to_all x3, waiting for transfers between devices, sum_parts(): lax.all_to_all(jnp.stack([own] * lax.axis_size(axis_name)), axis_name, 0, 0)  95.1 us
    all_to_all x1, blocking collectives, sum_parts(): lax.all_to_all(jnp.stack([own] * lax.axis_size(axis_name)), axis_name, 0, 0)  51.2 us
    all_gather x1, waiting for transfers between devices, on_device(): lax.all_gather(w_down, 'dp', axis=1, tiled=True)  47 us
    all_gather x1, waiting for transfers between devices, on_device(): lax.all_gather(w_up, 'dp', axis=0, tiled=True)  43.4 us
    all_gather x1, waiting for transfers between devices, on_device(): lax.all_gather(w_query, 'dp', axis=0, tiled=True)  26.1 us
    all_gather x1, waiting for transfers between devices, on_device(): lax.all_gather(w_key, 'dp', axis=0, tiled=True)  26 us
  transfers between devices with their start and end apart: 21, of which 17 were waited for; matrix products, arithmetic and copies ran while one was open for 11% of the time, Pallas kernels for 0%

profile of v1, /device:TPU:0, one launch (start us, length us, event | category | flops | bytes accessed | tf_op | source)
XLA Modules:
  0.0 1103.7 jit_solution(4844566471739694240)
XLA Ops:
  14.4 26.0 %all-gather.12.cloned.1.call-done = bf16[2048,512]{1,0:T(8,128)(2,1)} async-done(((bf16[256,512]{1,0:T(8,128)(2,1)}), bf16[2048,512]{1,0:T(8,128)(2,1)}) %all-gather.12.cloned.1.call-update) | async-done | bytes 2097168 | tf_op jit(solution)/shard_map/all_gather | solution.py:144
  44.0 26.1 %all-gather.10.cloned.1.call-done = bf16[2048,512]{1,0:T(8,128)(2,1)} async-done(((bf16[256,512]{1,0:T(8,128)(2,1)}), bf16[2048,512]{1,0:T(8,128)(2,1)}) %all-gather.10.cloned.1.call-update) | async-done | bytes 2097168 | tf_op jit(solution)/shard_map/all_gather | solution.py:143
  73.7 11.7 %all-reduce.2 = (f32[512]{0:T(512)S(1)}, f32[512]{0:T(512)S(1)}) all-reduce(f32[512]{0:T(512)S(1)} %get-tuple-element.81, f32[512]{0:T(512)S(1)} %get-tuple-element.83), channel_id=1, replica_groups=mesh['dp'=8,'mp'=4] {'mp'}, use_global_device_ids=true, to_apply=%region_5.6 | all-reduce | flops 1024 | bytes 8192 | tf_op jit(solution)/shard_map/psum | solution.py:163
  108.2 21.4 %all-gather.14.cloned.1.call-done = bf16[512,2048]{1,0:T(8,128)(2,1)} async-done(((bf16[512,256]{1,0:T(8,128)(2,1)}), bf16[512,2048]{1,0:T(8,128)(2,1)}) %all-gather.14.cloned.1.call-update) | async-done | bytes 2097168 | tf_op jit(solution)/shard_map/all_gather | solution.py:146
  136.5 41.2 %reduce-scatter.12.cloned.1.call-done = bf16[128,2048]{1,0:T(8,128)(2,1)} async-done(((bf16[512,2048]{1,0:T(8,128)(2,1)}), bf16[128,2048]{1,0:T(8,128)(2,1)}) %reduce-scatter.12.cloned.1.call-update) | async-done | bytes 524304 | tf_op jit(solution)/shard_map/reduce_scatter | solution.py:115
  179.0 51.2 %all_to_all.20 = bf16[4,128,2048]{2,1,0:T(8,128)(2,1)S(1)} all-to-all(bf16[4,128,2048]{2,1,0:T(8,128)(2,1)S(1)} %stack.8), channel_id=1, replica_groups=mesh['dp'=8,'mp'=4] {'mp'}, dimensions={0} | all-to-all | bytes 4194304 | tf_op jit(solution)/shard_map/all_to_all | solution.py:117
  235.1 10.6 fusion.44
  245.7 43.4 %all-gather.18.cloned.1.call-done = bf16[2048,2048]{1,0:T(8,128)(2,1)} async-done(((bf16[256,2048]{1,0:T(8,128)(2,1)}), bf16[2048,2048]{1,0:T(8,128)(2,1)}) %all-gather.18.cloned.1.call-update) | async-done | bytes 8388624 | tf_op jit(solution)/shard_map/all_gather | solution.py:148
  289.1 10.8 multiply_convert_fusion.3
  299.9 47.0 %all-gather.20.cloned.1.call-done = bf16[2048,2048]{1,0:T(8,128)(2,1)} async-done(((bf16[2048,256]{1,0:T(8,128)(2,1)}), bf16[2048,2048]{1,0:T(8,128)(2,1)}) %all-gather.20.cloned.1.call-update) | async-done | bytes 8388624 | tf_op jit(solution)/shard_map/all_gather | solution.py:149
  356.7 43.8 %reduce-scatter.14.cloned.1.call-done = bf16[128,2048]{1,0:T(8,128)(2,1)} async-done(((bf16[512,2048]{1,0:T(8,128)(2,1)}), bf16[128,2048]{1,0:T(8,128)(2,1)}) %reduce-scatter.14.cloned.1.call-update) | async-done | bytes 524304 | tf_op jit(solution)/shard_map/reduce_scatter | solution.py:115
  408.4 47.3 %all-to-all-done.1 = bf16[4,128,2048]{2,1,0:T(8,128)(2,1)} async-done(((bf16[4,128,2048]{2,1,0:T(8,128)(2,1)}), bf16[4,128,2048]{2,1,0:T(8,128)(2,1)}, u32[]{:S(2)}, u32[]{:S(2)}) %all-to-all-start.1) | async-done | bytes 2097184 | tf_op jit(solution)/shard_map/all_to_all | solution.py:117
  463.9 12.3 %multiply_convert_fusion.1 = (bf16[512,2048]{1,0:T(8,128)(2,1)}, bf16[512,2048]{1,0:T(8,128)(2,1)}) fusion(f32[512,2048]{1,0:T(8,128)S(1)} %copy-done.42, f32[512,2048]{1,0:T(8,128)} %get-tuple-element.88, bf16[512,2048]{1,0:T(8,128)(2,1)S(1)} %fusion.7, bf16[2048,2048]{1,0:T(8,128)(2,1)} %all-gather.20.cloned.1.call-done), kind=kOutput, calls=%fused_computation.38 | convolution fusion | flops 4308598784 | bytes 23068672 | tf_op jit(solution)/shard_map/dot_general | solution.py:194
  493.4 42.8 %reduce-scatter.16.cloned.1.call-done = bf16[128,2048]{1,0:T(8,128)(2,1)} async-done(((bf16[512,2048]{1,0:T(8,128)(2,1)}), bf16[128,2048]{1,0:T(8,128)(2,1)}) %reduce-scatter.16.cloned.1.call-update) | async-done | bytes 524304 | tf_op jit(solution)/shard_map/reduce_scatter | solution.py:115
  543.6 47.9 %all-to-all-done.2 = bf16[4,128,2048]{2,1,0:T(8,128)(2,1)} async-done(((bf16[4,128,2048]{2,1,0:T(8,128)(2,1)}), bf16[4,128,2048]{2,1,0:T(8,128)(2,1)}, u32[]{:S(2)}, u32[]{:S(2)}) %all-to-all-start.2) | async-done | bytes 2097184 | tf_op jit(solution)/shard_map/all_to_all | solution.py:117
  625.2 10.2 all-reduce.1
  683.2 10.1 convolution_convert_fusion.2
  700.5 24.2 %all-reduce = (f32[512]{0:T(512)}, f32[512]{0:T(512)}, f32[2048]{0:T(1024)}, f32[2048]{0:T(1024)}) all-reduce(f32[512]{0:T(512)S(1)} %get-tuple-element.45, f32[512]{0:T(512)S(1)} %get-tuple-element.43, f32[2048]{0:T(1024)S(1)} %get-tuple-element.39, f32[2048]{0:T(1024)S(1)} %get-tuple-element.41), channel_id=1, replica_groups=mesh['dp'=8,'mp'=4] {'dp'}, use_global_device_ids=true, to_apply=%region_29.30 | all-reduce | flops 5120 | bytes 40960 | tf_op jit(solution)/shard_map/psum | solution.py:252
  732.6 42.6 %reduce-scatter.22.cloned.1.call-done = bf16[256,512]{0,1:T(8,128)(2,1)} async-done(((bf16[2048,512]{0,1:T(8,128)(2,1)}), bf16[256,512]{0,1:T(8,128)(2,1)}) %reduce-scatter.22.cloned.1.call-update) | async-done | bytes 262160 | tf_op jit(solution)/shard_map/reduce_scatter | solution.py:108
  777.1 42.4 %reduce-scatter.20.cloned.1.call-done = bf16[256,512]{0,1:T(8,128)(2,1)} async-done(((bf16[2048,512]{0,1:T(8,128)(2,1)}), bf16[256,512]{0,1:T(8,128)(2,1)}) %reduce-scatter.20.cloned.1.call-update) | async-done | bytes 262160 | tf_op jit(solution)/shard_map/reduce_scatter | solution.py:108
  821.4 42.4 %reduce-scatter.24.cloned.1.call-done = bf16[256,512]{0,1:T(8,128)(2,1)} async-done(((bf16[2048,512]{0,1:T(8,128)(2,1)}), bf16[256,512]{0,1:T(8,128)(2,1)}) %reduce-scatter.24.cloned.1.call-update) | async-done | bytes 262160 | tf_op jit(solution)/shard_map/reduce_scatter | solution.py:108
  865.7 72.8 %reduce-scatter.32.cloned.1.call-done = bf16[2048,256]{1,0:T(8,128)(2,1)} async-done(((bf16[2048,2048]{1,0:T(8,128)(2,1)}), bf16[2048,256]{1,0:T(8,128)(2,1)}) %reduce-scatter.32.cloned.1.call-update) | async-done | bytes 1048592 | tf_op jit(solution)/shard_map/reduce_scatter | solution.py:108
  941.2 72.2 %reduce-scatter.30.cloned.1.call-done = bf16[256,2048]{1,0:T(8,128)(2,1)} async-done(((bf16[2048,2048]{1,0:T(8,128)(2,1)}), bf16[256,2048]{1,0:T(8,128)(2,1)}) %reduce-scatter.30.cloned.1.call-update) | async-done | bytes 1048592 | tf_op jit(solution)/shard_map/reduce_scatter | solution.py:108
  1016.1 72.1 %reduce-scatter.28.cloned.1.call-done = bf16[256,2048]{1,0:T(8,128)(2,1)} async-done(((bf16[2048,2048]{1,0:T(8,128)(2,1)}), bf16[256,2048]{1,0:T(8,128)(2,1)}) %reduce-scatter.28.cloned.1.call-update) | async-done | bytes 1048592 | tf_op jit(solution)/shard_map/reduce_scatter | solution.py:108
  (214 shorter events, 215.4 us)
Async XLA Ops:
  7.2 33.2 %all-gather.12.cloned.1.call-start = ((), (), s32[]{:S(2)}) async-start(), calls=%async_computation.17 | async-start | bytes 2359296 | tf_op jit(solution)/shard_map/all_gather | solution.py:144
  7.9 62.2 %all-gather.10.cloned.1.call-start = ((), (), s32[]{:S(2)}) async-start(), calls=%async_computation.16 | async-start | bytes 2359296 | tf_op jit(solution)/shard_map/all_gather | solution.py:143
  8.7 94.3 %all-gather.8.cloned.1.call-start = ((), (), s32[]{:S(2)}) async-start(), calls=%async_computation.15 | async-start | bytes 2359296 | tf_op jit(solution)/shard_map/all_gather | solution.py:145
  9.4 120.3 %all-gather.14.cloned.1.call-start = ((), (), s32[]{:S(2)}) async-start(), calls=%async_computation.18 | async-start | bytes 2359296 | tf_op jit(solution)/shard_map/all_gather | solution.py:146
  10.0 167.7 %reduce-scatter.12.cloned.1.call-start = ((), (), s32[]{:S(2)}) async-start(), calls=%async_computation.19 | async-start | bytes 2621440 | tf_op jit(solution)/shard_map/reduce_scatter | solution.py:115
  133.9 101.2 %all-gather.16.cloned.1.call-start = ((), (), s32[]{:S(2)}) async-start(), calls=%async_computation.20 | async-start | bytes 9437184 | tf_op jit(solution)/shard_map/all_gather | solution.py:147
  134.5 154.6 %all-gather.18.cloned.1.call-start = ((), (), s32[]{:S(2)}) async-start(), calls=%async_computation.21 | async-start | bytes 9437184 | tf_op jit(solution)/shard_map/all_gather | solution.py:148
  135.2 211.6 %all-gather.20.cloned.1.call-start = ((), (), s32[]{:S(2)}) async-start(), calls=%async_computation.22 | async-start | bytes 9437184 | tf_op jit(solution)/shard_map/all_gather | solution.py:149
  136.0 94.6 %copy-start.32 = (f32[2048]{0:T(1024)S(1)}, f32[2048]{0:T(1024)}, u32[]{:S(2)}) copy-start(f32[2048]{0:T(1024)} %param.28) | copy-start | bytes 24580
  136.0 264.5 %reduce-scatter.14.cloned.1.call-start = ((), (), s32[]{:S(2)}) async-start(), calls=%async_computation.23 | async-start | bytes 2621440 | tf_op jit(solution)/shard_map/reduce_scatter | solution.py:115
  356.7 101.1 %copy-start = (bf16[512,2048]{1,0:T(8,128)(2,1)S(1)}, bf16[512,2048]{1,0:T(8,128)(2,1)}, u32[]{:S(2)}) copy-start(bf16[512,2048]{1,0:T(8,128)(2,1)} %param.16) | copy-start | bytes 6291460
  356.7 101.1 %copy-start.33 = (f32[2048]{0:T(1024)S(1)}, f32[2048]{0:T(1024)}, u32[]{:S(2)}) copy-start(f32[2048]{0:T(1024)} %param.29) | copy-start | bytes 24580
  403.1 52.6 %all-to-all-start.1 = ((bf16[4,128,2048]{2,1,0:T(8,128)(2,1)}), bf16[4,128,2048]{2,1,0:T(8,128)(2,1)}, u32[]{:S(2)}, u32[]{:S(2)}) async-start(bf16[4,128,2048]{2,1,0:T(8,128)(2,1)} %stack.9), calls=%async_computation.3 | async-start | bytes 4194304 | tf_op jit(solution)/shard_map/all_to_all | solution.py:117
  407.6 128.6 %reduce-scatter.16.cloned.1.call-start = ((), (), s32[]{:S(2)}) async-start(), calls=%async_computation.24 | async-start | bytes 2621440 | tf_op jit(solution)/shard_map/reduce_scatter | solution.py:115
  538.8 52.7 %all-to-all-start.2 = ((bf16[4,128,2048]{2,1,0:T(8,128)(2,1)}), bf16[4,128,2048]{2,1,0:T(8,128)(2,1)}, u32[]{:S(2)}, u32[]{:S(2)}) async-start(bf16[4,128,2048]{2,1,0:T(8,128)(2,1)} %stack.10), calls=%async_computation.5 | async-start | bytes 4194304 | tf_op jit(solution)/shard_map/all_to_all | solution.py:117
  543.3 150.0 %reduce-scatter.18.cloned.1.call-start = ((), (), s32[]{:S(2)}) async-start(), calls=%async_computation.25 | async-start | bytes 2621440 | tf_op jit(solution)/shard_map/reduce_scatter | solution.py:115
  645.2 85.6 %reduce-scatter.26.cloned.1.call-start = ((), (), s32[]{:S(2)}) async-start(), calls=%async_computation.29 | async-start | bytes 2359296 | tf_op jit(solution)/shard_map/reduce_scatter | solution.py:108
  649.5 125.7 %reduce-scatter.22.cloned.1.call-start = ((), (), s32[]{:S(2)}) async-start(), calls=%async_computation.27 | async-start | bytes 2359296 | tf_op jit(solution)/shard_map/reduce_scatter | solution.py:108
  653.9 165.6 %reduce-scatter.20.cloned.1.call-start = ((), (), s32[]{:S(2)}) async-start(), calls=%async_computation.26 | async-start | bytes 2359296 | tf_op jit(solution)/shard_map/reduce_scatter | solution.py:108
  658.2 205.6 %reduce-scatter.24.cloned.1.call-start = ((), (), s32[]{:S(2)}) async-start(), calls=%async_computation.28 | async-start | bytes 2359296 | tf_op jit(solution)/shard_map/reduce_scatter | solution.py:108
  662.5 275.9 %reduce-scatter.32.cloned.1.call-start = ((), (), s32[]{:S(2)}) async-start(), calls=%async_computation.32 | async-start | bytes 9437184 | tf_op jit(solution)/shard_map/reduce_scatter | solution.py:108
  672.8 340.5 %reduce-scatter.30.cloned.1.call-start = ((), (), s32[]{:S(2)}) async-start(), calls=%async_computation.31 | async-start | bytes 9437184 | tf_op jit(solution)/shard_map/reduce_scatter | solution.py:108
  682.9 405.2 %reduce-scatter.28.cloned.1.call-start = ((), (), s32[]{:S(2)}) async-start(), calls=%async_computation.30 | async-start | bytes 9437184 | tf_op jit(solution)/shard_map/reduce_scatter | solution.py:108
  695.9 395.0 %all-to-all-start.3 = ((bf16[4,128,2048]{2,1,0:T(8,128)(2,1)}), bf16[4,128,2048]{2,1,0:T(8,128)(2,1)}, u32[]{:S(2)}, u32[]{:S(2)}) async-start(bf16[4,128,2048]{2,1,0:T(8,128)(2,1)} %stack.11), calls=%async_computation.7 | async-start | bytes 4194304 | tf_op jit(solution)/shard_map/all_to_all | solution.py:117
  (41 other events, 289.2 us)
Sparse Core Ops, SparseCore 0:
  9.9 30.4 all-gather.11
  42.3 27.7 all-gather.9
  72.0 27.7 all-gather.7
  101.5 28.0 all-gather.13
  134.0 43.6 reduce-scatter.11
  179.4 53.4 all-gather.15
  234.8 54.2 all-gather.17
  291.0 55.8 all-gather.19
  356.8 43.6 reduce-scatter.13
  493.5 42.6 reduce-scatter.15
  645.3 41.7 reduce-scatter.17
  690.2 40.5 reduce-scatter.25
  734.1 41.0 reduce-scatter.21
  778.4 41.1 reduce-scatter.19
  822.6 41.1 reduce-scatter.23
  867.1 71.2 reduce-scatter.31
  941.8 71.5 reduce-scatter.29
  1016.6 71.4 reduce-scatter.27
